TPU v7x, 32 devices: a whole 2x2x4 slice. The times are simulated.
32 devices in a mesh: slab: 16 (over z, y, x), pencil: 2 (over core).
Axes of the slice: x: 2, y: 2, z: 4, core: 2. Of those that a mesh axis runs over, the one named last changes fastest.
Arguments:
- density: float32 [96, 768, 384], P('slab', 'pencil'), may hold values from 0 to 1
- cell_kind: int32 [96, 768, 384], P('slab', 'pencil'), may hold values from 0 to 2
- sharpness: float32 [1], replicated, may hold values from 48 to 96
- fraction: float32 [1], replicated, may hold values from 0.36 to 0.41
Outputs:
- physical: float32 [96, 768, 384], P('slab', 'pencil')
- threshold: float32 [1], replicated
Inputs may be any that keep to these rules, and one draw needn't show every extreme that they name: `cell_kind`: each cell is a design, void or solid cell.
All inputs are finite; a program needn't handle non-finite values.
Results may differ from a plain program's by a relative error of at most 0.0003.
Values sent between devices are 32-bit elements; how exact they have to be, the bound alone decides.
A program may use at most 128 MiB of HBM per device.

v0:
```python
import jax
import jax.numpy as jnp
from jax import lax
from jax.sharding import PartitionSpec as P

RADIUS = 5
ITERS = 3


def extended(x, sides, width):
    for axis, dim in sides:
        size, length = (lax.axis_size(axis), x.shape[dim])
        up = [(i, (i + 1) % size) for i in range(size - 1)]
        down = [(j, i) for i, j in up]
        last = lax.slice_in_dim(x, length - width, length, axis=dim)
        leading = lax.slice_in_dim(x, 0, width, axis=dim)
        before = lax.ppermute(last, axis, up)
        after = lax.ppermute(leading, axis, down)
        x = jnp.concatenate([before, x, after], axis=dim)
    return x


def filter_padded(padded, axis, length):
    total = None
    for offset in range(-RADIUS, RADIUS + 1):
        weight = float(RADIUS + 1 - abs(offset))
        piece = lax.slice_in_dim(padded, RADIUS + offset, RADIUS + offset + length, axis=axis)
        total = weight * piece if total is None else total + weight * piece
    return total


def coverage_local(count, start, whole):
    index = start + jnp.arange(count, dtype=jnp.int32)
    total = jnp.zeros((count,), jnp.float32)
    for offset in range(-RADIUS, RADIUS + 1):
        inside = ((index + offset >= 0) & (index + offset < whole)).astype(jnp.float32)
        total = total + float(RADIUS + 1 - abs(offset)) * inside
    return total


def project(filtered, cell_kind, beta, level):
    tangent = jnp.tanh(beta * (filtered - level))
    design = cell_kind == 0
    solid = cell_kind == 2
    values = jnp.where(design, 0.5 * (1.0 + tangent), jnp.where(solid, 1.0, 0.0))
    return (values, tangent, design)


def local(density, cell_kind, sharpness, fraction):
    depth, rows, cols = density.shape
    slabs = lax.axis_size("slab")
    pencils = lax.axis_size("pencil")
    padded = extended(density, (("slab", 0),), RADIUS)
    along_z = filter_padded(padded, 0, depth)
    widened = extended(along_z, (("pencil", 1),), RADIUS)
    along_y = filter_padded(widened, 1, rows)
    along_x = filter_padded(jnp.pad(along_y, ((0, 0), (0, 0), (RADIUS, RADIUS))), 2, cols)
    cover_z = coverage_local(depth, lax.axis_index("slab") * depth, depth * slabs)
    cover_y = coverage_local(rows, lax.axis_index("pencil") * rows, rows * pencils)
    cover_x = coverage_local(cols, jnp.int32(0), cols)
    cover = cover_z[:, None, None] * cover_y[None, :, None] * cover_x[None, None, :]
    filtered = along_x / cover
    beta = sharpness[0]
    cells = jnp.float32(depth * slabs * rows * pencils * cols)
    level = jnp.float32(0.5)
    for step in range(ITERS):
        values, tangent, design = project(filtered, cell_kind, beta, level)
        volume_part = jnp.sum(values)
        slope_part = jnp.sum(jnp.where(design, 0.5 * beta * (1.0 - tangent * tangent), 0.0))
        volume, slope_sum = lax.psum((volume_part, slope_part), ("slab", "pencil"))
        level = level + (volume - fraction[0] * cells) / (cells + slope_sum)
    values, tangent, design = project(filtered, cell_kind, beta, level)
    return (values, jnp.reshape(level, (1,)))


def solution(mesh):
    in_specs = (P("slab", "pencil", None), P("slab", "pencil", None), P(), P())
    out_specs = (P("slab", "pencil", None), P())
    return jax.shard_map(local, mesh=mesh, in_specs=in_specs, out_specs=out_specs, check_vma=False)
```

profile of v0, /device:TPU:0, one launch (start us, length us, event | category | flops | bytes accessed | tf_op | source)
XLA Modules:
  0.0 325.6 jit_solution(1593789662947194971)
XLA Ops:
  0.6 4.8 %fusion.142 = (f32[5,384,384]{2,1,0:T(8,128)S(1)}, f32[5,384,384]{2,1,0:T(8,128)}) fusion(f32[6,384,384]{2,1,0:T(8,128)} %param.4), kind=kLoop, calls=%fused_computation.216 | loop fusion | bytes 11796480 | tf_op jit(solution)/shard_map/slice | solution.py:15
  5.4 6.5 %collective-permute-start = (f32[5,384,384]{2,1,0:T(8,128)S(1)}, f32[5,384,384]{2,1,0:T(8,128)}, u32[]{:S(2)}, u32[]{:S(2)}) collective-permute-start(f32[5,384,384]{2,1,0:T(8,128)S(1)} %get-tuple-element.21), channel_id=1, source_target_pairs={{0,2},{2,4},{4,6},{6,8},{8,10},{10,12},{12,14},{14,16},{16,18},{18... | collective-permute-start | bytes 8847368 | tf_op jit(solution)/shard_map/ppermute | solution.py:17
  11.9 1.3 collective-permute-start.1
  13.2 0.1 broadcast_multiply_fusion
  13.3 123.3 %collective-permute-done = f32[5,384,384]{2,1,0:T(8,128)} collective-permute-done((f32[5,384,384]{2,1,0:T(8,128)S(1)}, f32[5,384,384]{2,1,0:T(8,128)}, u32[]{:S(2)}, u32[]{:S(2)}) %collective-permute-start) | collective-permute-done | bytes 2949152 | tf_op jit(solution)/shard_map/ppermute | solution.py:17
  136.6 2.0 constant_dynamic-update-slice_fusion.1
  138.7 2.6 constant_dynamic-update-slice_fusion
  141.3 0.0 collective-permute-done.1
  141.3 2.0 constant_dynamic-update-slice_fusion.2
  143.3 5.0 %slice_add_fusion = f32[6,384,384]{2,1,0:T(8,128)} fusion(f32[11,384,384]{2,1,0:T(8,128)S(1)} %constant_dynamic-update-slice_fusion.2, f32[11,384,384]{2,1,0:T(8,128)S(1)} %get-tuple-element.19, f32[6,384,384]{2,1,0:T(8,128)} %param.4), kind=kLoop, calls=%fused_computation.76 | loop fusion | flops 16809984 | bytes 42467328 | tf_op jit(solution)/shard_map/add | solution.py:28
  148.3 0.9 fusion.141
  149.2 1.3 collective-permute-start.2
  150.5 1.3 collective-permute-start.3
  153.2 0.0 copy-start
  153.2 0.0 collective-permute-done.2
  153.2 0.5 collective-permute-done.3
  153.7 21.1 %fusion.25 = f32[6,384,384]{2,1,0:T(8,128)S(1)} fusion(f32[6,5,384]{2,1,0:T(8,128)S(1)} %collective-permute-done.3, f32[6,5,384]{2,1,0:T(8,128)S(1)} %collective-permute-done.2, f32[6,384,384]{2,1,0:T(8,128)} %slice_add_fusion), kind=kLoop, calls=%fused_computation.47 | loop fusion | flops 25657344 | bytes 7170048 | tf_op jit(solution)/shard_map/add | solution.py:28
  174.8 0.0 copy-done
  174.8 11.4 %select_reduce_fusion.2 = (f32[]{:T(128)}, f32[]{:T(128)}, f32[6,384,384]{2,1,0:T(8,128)S(1)}, pred[6,384,384]{2,1,0:T(8,128)(4,1)}, pred[6,384,384]{2,1,0:T(8,128)(4,1)}) fusion(f32[]{:T(128)S(6)} %mul.332, f32[]{:T(128)} %bitcast.7, f32[384]{0:T(512)S(1)} %convert_add_fusion, f32[6,384]{1,0:T(8,128)S(1)} %broadcast_multiply_fusion, ...), kind=kLoop, calls=%fused_computation.98 | loop fusion | flops 30965760 | bytes 12397072 | tf_op jit(solution)/shard_map/reduce_sum | solution.py:69
  186.2 40.9 %all-reduce.3 = (f32[]{:T(128)}, f32[]{:T(128)}) all-reduce(f32[]{:T(128)} %get-tuple-element.7, f32[]{:T(128)} %get-tuple-element.6), channel_id=1, replica_groups=mesh['slab'=16,'pencil'=2] {'slab','pencil'}, use_global_device_ids=true, to_apply=%region_1.2 | all-reduce | flops 2 | bytes 16 | tf_op jit(solution)/shard_map/psum | solution.py:70
  228.4 4.0 %select_reduce_fusion.1 = (f32[]{:T(128)}, f32[]{:T(128)}) fusion(pred[6,384,384]{2,1,0:T(8,128)(4,1)} %get-tuple-element.16, f32[6,384,384]{2,1,0:T(8,128)S(1)} %get-tuple-element.14, f32[]{:T(128)S(6)} %add.701, f32[]{:T(128)S(6)} %mul.332, f32[]{:T(128)} %bitcast.6, pred[6,384,384]{2,1,0:T(8,128)(4,1)} %get-tuple-element.15), kind=kLoop, calls=%fused_computation.96 | loop fusion | flops 10616830 | bytes 5308436 | tf_op jit(solution)/shard_map/reduce_sum | solution.py:69
  232.4 40.2 %all-reduce.2 = (f32[]{:T(128)}, f32[]{:T(128)}) all-reduce(f32[]{:T(128)} %get-tuple-element.5, f32[]{:T(128)} %get-tuple-element.4), channel_id=1, replica_groups=mesh['slab'=16,'pencil'=2] {'slab','pencil'}, use_global_device_ids=true, to_apply=%region_5.6 | all-reduce | flops 2 | bytes 16 | tf_op jit(solution)/shard_map/psum | solution.py:70
  273.9 4.0 %select_reduce_fusion = (f32[]{:T(128)}, f32[]{:T(128)}) fusion(pred[6,384,384]{2,1,0:T(8,128)(4,1)} %get-tuple-element.16, f32[6,384,384]{2,1,0:T(8,128)S(1)} %get-tuple-element.14, f32[]{:T(128)S(6)} %add.704, f32[]{:T(128)S(6)} %mul.332, f32[]{:T(128)} %bitcast.5, pred[6,384,384]{2,1,0:T(8,128)(4,1)} %get-tuple-element.15), kind=kLoop, calls=%fused_computation.94 | loop fusion | flops 10616830 | bytes 5308436 | tf_op jit(solution)/shard_map/reduce_sum | solution.py:69
  277.9 40.8 %all-reduce.1 = (f32[]{:T(128)}, f32[]{:T(128)}) all-reduce(f32[]{:T(128)} %get-tuple-element.3, f32[]{:T(128)} %get-tuple-element.2), channel_id=1, replica_groups=mesh['slab'=16,'pencil'=2] {'slab','pencil'}, use_global_device_ids=true, to_apply=%region_9.10 | all-reduce | flops 2 | bytes 16 | tf_op jit(solution)/shard_map/psum | solution.py:70
  320.0 4.5 %select_select_fusion = f32[6,384,384]{2,1,0:T(8,128)} fusion(pred[6,384,384]{2,1,0:T(8,128)(4,1)} %get-tuple-element.16, pred[6,384,384]{2,1,0:T(8,128)(4,1)} %get-tuple-element.15, f32[6,384,384]{2,1,0:T(8,128)S(1)} %get-tuple-element.14, f32[]{:T(128)} %add.707, f32[]{:T(128)} %bitcast.3), kind=kLoop, calls=%fused_computation.18 | loop fusion | flops 5308416 | bytes 8847368 | tf_op jit(solution)/shard_map/jit(_where)/select_n | solution.py:45
  (3 shorter events, 0.1 us)
Async XLA Ops:
  5.4 131.2 %collective-permute-start = (f32[5,384,384]{2,1,0:T(8,128)S(1)}, f32[5,384,384]{2,1,0:T(8,128)}, u32[]{:S(2)}, u32[]{:S(2)}) collective-permute-start(f32[5,384,384]{2,1,0:T(8,128)S(1)} %get-tuple-element.21), channel_id=1, source_target_pairs={{0,2},{2,4},{4,6},{6,8},{8,10},{10,12},{12,14},{14,16},{16,18},{18... | collective-permute-start | bytes 8847368 | tf_op jit(solution)/shard_map/ppermute | solution.py:17
  11.9 129.4 %collective-permute-start.1 = (f32[5,384,384]{2,1,0:T(8,128)}, f32[5,384,384]{2,1,0:T(8,128)}, u32[]{:S(2)}, u32[]{:S(2)}) collective-permute-start(f32[5,384,384]{2,1,0:T(8,128)} %get-tuple-element.22), channel_id=1, source_target_pairs={{2,0},{4,2},{6,4},{8,6},{10,8},{12,10},{14,12},{16,14},{18,16},{20... | collective-permute-start | bytes 8847368 | tf_op jit(solution)/shard_map/ppermute | solution.py:18
  149.2 3.9 %collective-permute-start.2 = (f32[6,5,384]{2,1,0:T(8,128)S(1)}, f32[6,5,384]{2,1,0:T(8,128)S(1)}, u32[]{:S(2)}, u32[]{:S(2)}) collective-permute-start(f32[6,5,384]{2,1,0:T(8,128)S(1)} %get-tuple-element.17), channel_id=1, source_target_pairs={{0,1},{2,3},{4,5},{6,7},{8,9},{10,11},{12,13},{14,15},{16,17},{18,... | collective-permute-start | bytes 138248 | tf_op jit(solution)/shard_map/ppermute | solution.py:17
  150.5 3.2 collective-permute-start.3
  153.2 21.6 %copy-start = (s32[6,384,384]{2,1,0:T(8,128)S(1)}, s32[6,384,384]{2,1,0:T(8,128)}, u32[]{:S(2)}) copy-start(s32[6,384,384]{2,1,0:T(8,128)} %param.5) | copy-start | bytes 10616836
where the time goes:
time: 326 us
  waiting for transfers between devices  124 us (38%)
  blocking collectives  122 us (37%)
  other arithmetic  50 us (15%)
  local copies, waits for them, and re-layouts  12.4 us (4%)
  starting transfers between devices  10.3 us (3%)
  between operations  7.2 us (2%)
    ppermute x2, waiting for transfers between devices, extended(): before = lax.ppermute(last, axis, up)  123 us
    psum x3, blocking collectives, local(): volume, slope_sum = lax.psum((volume_part, slope_part), ('slab', 'pencil'))  122 us
    add x2, other arithmetic, filter_padded(): total = weight * piece if total is None else total + weight * piece  26 us
    reduce_sum x3, other arithmetic, local(): jnp.sum(jnp.where(design, 0.5 * beta * (1.0 - tangent * tangent), 0.0))  19.4 us
    ppermute x2, starting transfers between devices, extended(): before = lax.ppermute(last, axis, up)  7.76 us
  transfers between devices with their start and end apart: 4, of which 2 were waited for; matrix products, arithmetic and copies ran while one was open for 1% of the time, Pallas kernels for 0%

commit v1 on v0

v1 whole, which is shorter than its diff:
```python
import functools

import jax
import jax.numpy as jnp
from jax import lax
from jax.experimental import pallas as pl
from jax.experimental.pallas import tpu as pltpu
from jax.sharding import PartitionSpec as P

RADIUS = 5
ITERS = 3
CHUNK = 16
PAD = 8
WINDOW = 4
LAG = 2
LANES = 128
FAR = 1.0e6
MESH = pl.DeviceIdType.MESH


def box(values):
    pairs = [a + b for a, b in zip(values[:-1], values[1:])]
    return [pairs[k] + pairs[k + 2] + pairs[k + 4] for k in range(len(values) - RADIUS)]


def triangle(k):
    k = jnp.maximum(k, 0)
    return (k * (k + 1)) // 2


def coverage(index, whole):
    full = (RADIUS + 1) * (RADIUS + 1)
    return (full - triangle(RADIUS - index) - triangle(RADIUS + 1 + index - whole)).astype(jnp.float32)


def split(x):
    high = x.astype(jnp.bfloat16)
    return high, (x - high.astype(jnp.float32)).astype(jnp.bfloat16)


def band(shape, shift):
    row = lax.broadcasted_iota(jnp.int32, shape, 0)
    col = lax.broadcasted_iota(jnp.int32, shape, 1)
    return jnp.maximum(RADIUS + 1 - jnp.abs(col - shift - row), 0).astype(jnp.float32).astype(jnp.bfloat16)


def folded(x):
    tiles = [
        x[i : i + 8, j : j + LANES] for i in range(0, x.shape[0], 8) for j in range(0, x.shape[1], LANES)
    ]
    while len(tiles) > 1:
        tiles = [sum(tiles[i : i + 2][1:], tiles[i]) for i in range(0, len(tiles), 2)]
    return tiles[0]


def kernel(slabs, pencils, beta_ref, fraction_ref, density, kind, coded_out, level_out, own, near, far, kinds,
           along_z, coded, x_band, acc, parts, x_send, x_recv, f_send, f_recv, h_send, h_recv, local_sem,
           r_send, r_recv):
    depth, rows, cols = density.shape
    steps = rows // CHUNK
    slab = lax.axis_index("slab")
    pencil = lax.axis_index("pencil")
    even = slab % 2 == 0
    first = pencil == 0
    devices = slabs * pencils
    me = slab * pencils + pencil

    barrier = pltpu.get_barrier_semaphore()

    @pl.loop(1, devices)
    def _(k):
        other = (me + k) % devices
        pl.semaphore_signal(barrier, inc=1, device_id=(other // pencils, other % pencils), device_id_type=MESH)

    partner = slab + jnp.where(even, 1, -1)
    target = slab + jnp.where(even, 2, -2)
    source = slab - jnp.where(even, 2, -2)
    has_target = (target >= 0) & (target < slabs)
    has_source = (source >= 0) & (source < slabs)
    target = jnp.clip(target, 0, slabs - 1)
    sibling = 1 - pencil
    halo = pl.multiple_of(jnp.where(first, PAD + rows, 0), 8)
    edge = pl.multiple_of(jnp.where(first, 0, PAD + rows), 8)
    there = pl.multiple_of(jnp.where(first, 0, PAD + rows), 8)
    mine = pl.multiple_of(jnp.where(first, rows, PAD), 8)

    def row_of(k):
        return pl.multiple_of(jnp.where(first, steps - 1 - k, k) * CHUNK, CHUNK)

    def x_copy(k):
        r = row_of(k)
        return pltpu.make_async_remote_copy(
            density.at[:, pl.ds(r, CHUNK), :], near.at[:, pl.ds(r + PAD, CHUNK), :],
            x_send.at[k], x_recv.at[k], device_id=(partner, pencil), device_id_type=MESH)

    def f_copy(k):
        r = row_of(k)
        start = jnp.where(even, depth - RADIUS, 0)
        return pltpu.make_async_remote_copy(
            near.at[pl.ds(start, RADIUS), pl.ds(r + PAD, CHUNK), :], far.at[:, pl.ds(r + PAD, CHUNK), :],
            f_send.at[k], f_recv.at[k], device_id=(target, pencil), device_id_type=MESH)

    def halo_copy(index, src, dst):
        return pltpu.make_async_remote_copy(
            src, dst, h_send.at[index], h_recv.at[index], device_id=(slab, sibling), device_id_type=MESH)

    own_row = pl.multiple_of(jnp.where(first, rows - PAD, 0), 8)
    own_halo = halo_copy(0, density.at[:, pl.ds(own_row, PAD), :], own.at[:, pl.ds(there, PAD), :])
    near_halo = halo_copy(1, near.at[:, pl.ds(mine, PAD), :], near.at[:, pl.ds(there, PAD), :])
    far_halo = halo_copy(2, far.at[:, pl.ds(mine, PAD), :], far.at[:, pl.ds(there, PAD), :])
    own_load = pltpu.make_async_copy(density, own.at[:, pl.ds(PAD, rows), :], local_sem.at[0])
    kind_load = pltpu.make_async_copy(kind, kinds, local_sem.at[1])
    coded_store = pltpu.make_async_copy(coded, coded_out, local_sem.at[2])

    pl.semaphore_wait(barrier, devices - 1)
    for k in range(min(WINDOW, steps)):
        x_copy(k).start()
    own_halo.start()
    own_load.start()
    kind_load.start()

    x_band[...] = band((cols, cols), 0)
    acc[...] = jnp.zeros_like(acc)
    along_z[:, pl.ds(edge, PAD), :] = jnp.zeros((depth, PAD, cols), jnp.float32)

    @pl.when(jnp.logical_not(has_source))
    def _():
        @pl.loop(0, RADIUS)
        def _(k):
            far[k] = jnp.zeros(far.shape[1:], jnp.float32)

    beta = beta_ref[0]

    def filter_z(start, count):
        for r in range(0, count, 8):
            for c in range(0, cols, LANES):
                at = (pl.ds(pl.multiple_of(start + r, 8), 8), pl.ds(c, LANES))
                values = [far[jnp.where(even, m, RADIUS - 1 - m), at[0], at[1]] for m in range(RADIUS)]
                values += [own[jnp.where(even, i, depth - 1 - i), at[0], at[1]] for i in range(depth)]
                values += [near[jnp.where(even, i, depth - 1 - i), at[0], at[1]] for i in range(RADIUS)]
                for i, out in enumerate(box(box(values))):
                    along_z[jnp.where(even, i, depth - 1 - i), at[0], at[1]] = out

    def filter_yx(j):
        r = row_of(j)
        y_band = band((CHUNK, CHUNK + 2 * PAD), PAD)
        pieces = []
        for layer in range(depth):
            high, low = split(along_z[layer, pl.ds(r, CHUNK + 2 * PAD), :])
            pieces.append(jnp.dot(y_band, high, preferred_element_type=jnp.float32)
                          + jnp.dot(y_band, low, preferred_element_type=jnp.float32))
        high, low = split(jnp.concatenate(pieces, axis=0))
        smoothed = (jnp.dot(high, x_band[...], preferred_element_type=jnp.float32)
                    + jnp.dot(low, x_band[...], preferred_element_type=jnp.float32))
        row = lax.broadcasted_iota(jnp.int32, (CHUNK, cols), 0) + (pencil * rows + r)
        col = lax.broadcasted_iota(jnp.int32, (CHUNK, cols), 1)
        cover_y = coverage(row, rows * pencils)
        cover_x = coverage(col, cols)
        for layer in range(depth):
            depth_index = jnp.full((1, cols), slab * depth + layer, jnp.int32)
            cover = coverage(depth_index, slabs * depth) * cover_y * cover_x
            filtered = smoothed[layer * CHUNK : (layer + 1) * CHUNK] / cover
            which = kinds[layer, pl.ds(r, CHUNK), :]
            value = jnp.where(which == 0, filtered, jnp.where(which == 2, FAR, -FAR))
            coded[layer, pl.ds(r, CHUNK), :] = value
            tangent = jnp.tanh(beta * (value - 0.5))
            acc[0] += folded(tangent)
            acc[1] += folded(1.0 - tangent * tangent)

    @pl.loop(0, steps + LAG + 1)
    def _(k):
        @pl.when(k < steps)
        def _():
            x_copy(k).wait_recv()

            @pl.when(has_target)
            def _():
                f_copy(k).start()

            @pl.when(k == 0)
            def _():
                near_halo.start()

        @pl.when(k + WINDOW < steps)
        def _():
            x_copy(k + WINDOW).start()

        @pl.when((k >= LAG) & (k < steps + LAG))
        def _():
            @pl.when(has_source)
            def _():
                f_copy(k - LAG).wait_recv()

                @pl.when(k == LAG)
                def _():
                    far_halo.start()

            @pl.when(k == LAG)
            def _():
                own_load.wait()
                kind_load.wait()

            filter_z(row_of(k - LAG) + PAD, CHUNK)

        @pl.when(k == LAG + 1)
        def _():
            own_halo.wait_recv()
            near_halo.wait_recv()

            @pl.when(has_source)
            def _():
                far_halo.wait_recv()

            filter_z(halo, PAD)

        @pl.when(k >= LAG + 1)
        def _():
            filter_yx(k - LAG - 1)

    coded_store.start()

    cells = float(devices) * float(depth * rows * cols)
    level = jnp.full((1, 1), 0.5, jnp.float32)
    for step in range(ITERS):
        if step:
            center = jnp.broadcast_to(level, (8, cols))

            def body(i, carry):
                total, bend = carry
                for layer in range(depth):
                    tangent = jnp.tanh(beta * (coded[layer, pl.ds(pl.multiple_of(i * 8, 8), 8), :] - center))
                    total = total + tangent
                    bend = bend + (1.0 - tangent * tangent)
                return total, bend

            zero = jnp.zeros((8, cols), jnp.float32)
            total, bend = lax.fori_loop(0, rows // 8, body, (zero, zero))
            total, bend = folded(total), folded(bend)
        else:
            total, bend = acc[0], acc[1]
        parts[step, me] = jnp.concatenate(
            [jnp.sum(total, axis=0, keepdims=True), jnp.sum(bend, axis=0, keepdims=True)], axis=0)

        @pl.loop(1, devices)
        def _(k):
            other = (me + k) % devices
            pltpu.make_async_remote_copy(
                parts.at[step, me], parts.at[step, me], r_send.at[step], r_recv.at[step],
                device_id=(other // pencils, other % pencils), device_id_type=MESH).start()

        most = parts.at[step, pl.ds(0, devices - 1)]
        pltpu.make_async_copy(most, most, r_recv.at[step]).wait()
        both = jnp.sum(jnp.sum(parts[step], axis=0), axis=1, keepdims=True)
        volume = 0.5 * (cells + both[0:1])
        slope = cells + 0.5 * beta * both[1:2]
        level = level + (volume - fraction_ref[0] * cells) / slope
    level_out[...] = jnp.broadcast_to(level, level_out.shape)

    @pl.loop(0, steps)
    def _(k):
        x_copy(k).wait_send()

        @pl.when(has_target)
        def _():
            f_copy(k).wait_send()

    own_halo.wait_send()
    near_halo.wait_send()

    @pl.when(has_source)
    def _():
        far_halo.wait_send()

    for step in range(ITERS):
        most = parts.at[step, pl.ds(0, devices - 1)]
        pltpu.make_async_copy(most, most, r_send.at[step]).wait()
    coded_store.wait()


def solution(mesh):
    slabs, pencils = mesh.shape["slab"], mesh.shape["pencil"]

    def local(density, cell_kind, sharpness, fraction):
        depth, rows, cols = density.shape
        steps = rows // CHUNK
        wide = rows + 2 * PAD
        coded, level = pl.pallas_call(
            functools.partial(kernel, slabs, pencils),
            out_shape=(jax.ShapeDtypeStruct(density.shape, jnp.float32), jax.ShapeDtypeStruct((1, LANES), jnp.float32)),
            in_specs=[pl.BlockSpec(memory_space=pltpu.SMEM)] * 2 + [pl.BlockSpec(memory_space=pl.ANY)] * 2,
            out_specs=(pl.BlockSpec(memory_space=pl.ANY), pl.BlockSpec(memory_space=pltpu.VMEM)),
            scratch_shapes=[
                pltpu.VMEM((depth, wide, cols), jnp.float32),
                pltpu.VMEM((depth, wide, cols), jnp.float32),
                pltpu.VMEM((RADIUS, wide, cols), jnp.float32),
                pltpu.VMEM((depth, rows, cols), jnp.int32),
                pltpu.VMEM((depth, wide, cols), jnp.float32),
                pltpu.VMEM((depth, rows, cols), jnp.float32),
                pltpu.VMEM((cols, cols), jnp.bfloat16),
                pltpu.VMEM((2, 8, LANES), jnp.float32),
                pltpu.VMEM((ITERS, slabs * pencils, 2, LANES), jnp.float32),
                pltpu.SemaphoreType.DMA((steps,)),
                pltpu.SemaphoreType.DMA((steps,)),
                pltpu.SemaphoreType.DMA((steps,)),
                pltpu.SemaphoreType.DMA((steps,)),
                pltpu.SemaphoreType.DMA((3,)),
                pltpu.SemaphoreType.DMA((3,)),
                pltpu.SemaphoreType.DMA((3,)),
                pltpu.SemaphoreType.DMA((ITERS,)),
                pltpu.SemaphoreType.DMA((ITERS,)),
            ],
            compiler_params=pltpu.CompilerParams(
                collective_id=0, has_side_effects=True, vmem_limit_bytes=40 * 1024 * 1024),
        )(sharpness, fraction, density, cell_kind)
        threshold = level[0, :1]
        physical = 0.5 * (1.0 + jnp.tanh(sharpness[0] * (coded - threshold[0])))
        return physical, threshold

    in_specs = (P("slab", "pencil", None), P("slab", "pencil", None), P(), P())
    out_specs = (P("slab", "pencil", None), P())
    return jax.shard_map(local, mesh=mesh, in_specs=in_specs, out_specs=out_specs, check_vma=False)
```

time: 326 us -> 117 us (0.36)
  waiting for transfers between devices: 124 us -> 0 us
  blocking collectives: 122 us -> 0 us
  Pallas kernels: 0 us -> 108 us
  other arithmetic: 50 us -> 2.4 us
  starting transfers between devices: 10.3 us -> 0 us
  local copies, waits for them, and re-layouts: 12.4 us -> 3.99 us
  between operations: 7.2 us -> 3.1 us
    ppermute x4 -> x0, waiting for transfers between devices: 124 us -> none  [the longest x2 123 us: extended(): before = lax.ppermute(last, axis, up)]
    psum x3 -> x0, blocking collectives: 122 us -> none  [local(): volume, slope_sum = lax.psum((volume_part, slope_part), ('slab', 'pencil'))]
    pallas_call x0 -> x1, Pallas kernels: none -> 108 us  [local(): pl.pallas_call(functools.partial(kernel, slabs, pencils), out_shape=(jax....]
    add x5 -> x0, other arithmetic: 26.1 us -> none  [the longest x2 26 us: filter_padded(): total = weight * piece if total is None else total + weight * piece]
    reduce_sum x3 -> x0, other arithmetic: 19.4 us -> none  [local(): jnp.sum(jnp.where(design, 0.5 * beta * (1.0 - tangent * tangent), 0.0))]
    ppermute x4 -> x0, starting transfers between devices: 10.3 us -> none  [the longest x2 7.76 us: extended(): before = lax.ppermute(last, axis, up)]
    slice x2 -> x0, local copies, waits for them, and re-layouts: 5.72 us -> none  [extended(): last = lax.slice_in_dim(x, length - width, length, axis=dim)]
    concatenate x2 -> x0, local copies, waits for them, and re-layouts: 4.66 us -> none  [extended(): x = jnp.concatenate([before, x, after], axis=dim)]
  transfers between devices with their start and end apart: 4 -> 0, of which waited for: 2 -> 0; matrix products, arithmetic and copies ran while one was open for 1% -> 0% of each run, Pallas kernels for 0% -> 0%
where the time goes in v1:
time: 117 us
  Pallas kernels  108 us (92%)
  local copies, waits for them, and re-layouts  3.99 us (3%)
  between operations  3.1 us (3%)
  other arithmetic  2.4 us (2%)
    pallas_call x1, Pallas kernels, local(): pl.pallas_call(functools.partial(kernel, slabs, pencils), out_shape=(jax....  108 us
    unnamed x4, local copies, waits for them, and re-layouts  3.99 us
    mul x1, other arithmetic, local(): physical = 0.5 * (1.0 + jnp.tanh(sharpness[0] * (coded - threshold[0])))  2.4 us

profile of v1, /device:TPU:0, one launch (start us, length us, event | category | flops | bytes accessed | tf_op | source)
XLA Modules:
  0.0 117.0 jit_solution(18390224421540922115)
XLA Ops:
  1.9 0.0 copy-start
  1.9 2.0 %copy-done = f32[6,384,384]{2,1,0:T(8,128)S(1)} copy-done((f32[6,384,384]{2,1,0:T(8,128)S(1)}, f32[6,384,384]{2,1,0:T(8,128)}, u32[]{:S(2)}) %copy-start) | copy-done | bytes 3538968
  3.9 0.0 copy-start.1
  3.9 2.0 %copy-done.1 = s32[6,384,384]{2,1,0:T(8,128)S(1)} copy-done((s32[6,384,384]{2,1,0:T(8,128)S(1)}, s32[6,384,384]{2,1,0:T(8,128)}, u32[]{:S(2)}) %copy-start.1) | copy-done | bytes 3538968
  5.9 107.5 %shard_map.59 = (f32[6,384,384]{2,1,0:T(8,128)S(1)}, f32[1,128]{1,0:T(1,128)S(1)}) custom-call(f32[1]{0:T(128)} %copy.7.beta_ref, f32[1]{0:T(128)S(6)} %copy.8.fraction_ref, f32[6,384,384]{2,1,0:T(8,128)S(1)} %copy-done, s32[6,384,384]{2,1,0:T(8,128)S(1)} %copy-done.1), custom_call_target="tpu_custom_call" | custom-call | tf_op jit(solution)/shard_map/pallas_call | solution.py:287
  113.4 2.4 %add_multiply_fusion = f32[6,384,384]{2,1,0:T(8,128)} fusion(f32[6,384,384]{2,1,0:T(8,128)S(1)} %get-tuple-element.4, f32[]{:T(128)S(1)} %bitcast.5, f32[]{:T(128)} %bitcast.4), kind=kLoop, calls=%fused_computation | loop fusion | flops 3538944 | bytes 7077896 | tf_op jit(solution)/shard_map/mul | solution.py:316
Async XLA Ops:
  1.9 2.0 %copy-start = (f32[6,384,384]{2,1,0:T(8,128)S(1)}, f32[6,384,384]{2,1,0:T(8,128)}, u32[]{:S(2)}) copy-start(f32[6,384,384]{2,1,0:T(8,128)} %density.1) | copy-start | bytes 10616836
  3.9 2.0 %copy-start.1 = (s32[6,384,384]{2,1,0:T(8,128)S(1)}, s32[6,384,384]{2,1,0:T(8,128)}, u32[]{:S(2)}) copy-start(s32[6,384,384]{2,1,0:T(8,128)} %kind.1) | copy-start | bytes 10616836

commit v2 on v1

--- a/solution.py
+++ b/solution.py
@@ -12,7 +12,7 @@
 CHUNK = 16
 PAD = 8
 WINDOW = 4
-LAG = 2
+LEAD = 8
 LANES = 128
 FAR = 1.0e6
 MESH = pl.DeviceIdType.MESH
@@ -53,11 +53,13 @@
     return tiles[0]
 
 
-def kernel(slabs, pencils, beta_ref, fraction_ref, density, kind, coded_out, level_out, own, near, far, kinds,
-           along_z, coded, x_band, acc, parts, x_send, x_recv, f_send, f_recv, h_send, h_recv, local_sem,
+def kernel(slabs, pencils, beta_ref, fraction_ref, density, kind, coded, level_out, own, near, far, kinds,
+           along_z, x_band, acc, parts, x_send, x_recv, b_send, b_recv, f_send, f_recv, h_send, h_recv, local_sem,
            r_send, r_recv):
     depth, rows, cols = density.shape
     steps = rows // CHUNK
+    lead = min(LEAD, steps)
+    lag = lead + 1
     slab = lax.axis_index("slab")
     pencil = lax.axis_index("pencil")
     even = slab % 2 == 0
@@ -89,9 +91,17 @@
 
     def x_copy(k):
         r = row_of(k)
+        layers = pl.ds(jnp.where(even, 0, depth - RADIUS), RADIUS)
         return pltpu.make_async_remote_copy(
-            density.at[:, pl.ds(r, CHUNK), :], near.at[:, pl.ds(r + PAD, CHUNK), :],
+            density.at[layers, pl.ds(r, CHUNK), :], near.at[layers, pl.ds(r + PAD, CHUNK), :],
             x_send.at[k], x_recv.at[k], device_id=(partner, pencil), device_id_type=MESH)
+
+    def b_copy(k):
+        r = row_of(k)
+        layers = pl.ds(jnp.where(even, RADIUS, 0), depth - RADIUS)
+        return pltpu.make_async_remote_copy(
+            density.at[layers, pl.ds(r, CHUNK), :], near.at[layers, pl.ds(r + PAD, CHUNK), :],
+            b_send.at[k], b_recv.at[k], device_id=(partner, pencil), device_id_type=MESH)
 
     def f_copy(k):
         r = row_of(k)
@@ -110,14 +120,13 @@
     far_halo = halo_copy(2, far.at[:, pl.ds(mine, PAD), :], far.at[:, pl.ds(there, PAD), :])
     own_load = pltpu.make_async_copy(density, own.at[:, pl.ds(PAD, rows), :], local_sem.at[0])
     kind_load = pltpu.make_async_copy(kind, kinds, local_sem.at[1])
-    coded_store = pltpu.make_async_copy(coded, coded_out, local_sem.at[2])
-
+
+    own_load.start()
+    kind_load.start()
     pl.semaphore_wait(barrier, devices - 1)
     for k in range(min(WINDOW, steps)):
         x_copy(k).start()
     own_halo.start()
-    own_load.start()
-    kind_load.start()
 
     x_band[...] = band((cols, cols), 0)
     acc[...] = jnp.zeros_like(acc)
@@ -167,7 +176,7 @@
             acc[0] += folded(tangent)
             acc[1] += folded(1.0 - tangent * tangent)
 
-    @pl.loop(0, steps + LAG + 1)
+    @pl.loop(0, steps + lag + 1)
     def _(k):
         @pl.when(k < steps)
         def _():
@@ -177,32 +186,44 @@
             def _():
                 f_copy(k).start()
 
-            @pl.when(k == 0)
+        @pl.when(k + WINDOW < steps)
+        def _():
+            x_copy(k + WINDOW).start()
+
+            @pl.when(k + WINDOW >= lead)
+            def _():
+                b_copy(k + WINDOW - lead).start()
+
+        @pl.when(k + WINDOW == steps)
+        def _():
+            @pl.loop(max(steps - lead, 0), steps)
+            def _(j):
+                b_copy(j).start()
+
+        @pl.when((k >= lag) & (k < steps + lag))
+        def _():
+            b_copy(k - lag).wait_recv()
+
+            @pl.when(k == lag)
             def _():
                 near_halo.start()
 
-        @pl.when(k + WINDOW < steps)
-        def _():
-            x_copy(k + WINDOW).start()
-
-        @pl.when((k >= LAG) & (k < steps + LAG))
-        def _():
             @pl.when(has_source)
             def _():
-                f_copy(k - LAG).wait_recv()
-
-                @pl.when(k == LAG)
+                f_copy(k - lag).wait_recv()
+
+                @pl.when(k == lag)
                 def _():
                     far_halo.start()
 
-            @pl.when(k == LAG)
+            @pl.when(k == lag)
             def _():
                 own_load.wait()
                 kind_load.wait()
 
-            filter_z(row_of(k - LAG) + PAD, CHUNK)
-
-        @pl.when(k == LAG + 1)
+            filter_z(row_of(k - lag) + PAD, CHUNK)
+
+        @pl.when(k == lag + 1)
         def _():
             own_halo.wait_recv()
             near_halo.wait_recv()
@@ -213,11 +234,9 @@
 
             filter_z(halo, PAD)
 
-        @pl.when(k >= LAG + 1)
-        def _():
-            filter_yx(k - LAG - 1)
-
-    coded_store.start()
+        @pl.when(k >= lag + 1)
+        def _():
+            filter_yx(k - lag - 1)
 
     cells = float(devices) * float(depth * rows * cols)
     level = jnp.full((1, 1), 0.5, jnp.float32)
@@ -241,12 +260,20 @@
         parts[step, me] = jnp.concatenate(
             [jnp.sum(total, axis=0, keepdims=True), jnp.sum(bend, axis=0, keepdims=True)], axis=0)
 
-        @pl.loop(1, devices)
-        def _(k):
-            other = (me + k) % devices
+        def send(there, core):
             pltpu.make_async_remote_copy(
                 parts.at[step, me], parts.at[step, me], r_send.at[step], r_recv.at[step],
-                device_id=(other // pencils, other % pencils), device_id_type=MESH).start()
+                device_id=(there, core), device_id_type=MESH).start()
+
+        def send_all(k, carry):
+            there = slab + (slabs - k)
+            there = there - jnp.where(there >= slabs, slabs, 0)
+            for core in range(pencils):
+                send(there, core)
+            return carry
+
+        lax.fori_loop(1, slabs, send_all, 0, unroll=5 if slabs % 5 == 1 else 1)
+        send(slab, sibling)
 
         most = parts.at[step, pl.ds(0, devices - 1)]
         pltpu.make_async_copy(most, most, r_recv.at[step]).wait()
@@ -259,6 +286,7 @@
     @pl.loop(0, steps)
     def _(k):
         x_copy(k).wait_send()
+        b_copy(k).wait_send()
 
         @pl.when(has_target)
         def _():
@@ -274,7 +302,6 @@
     for step in range(ITERS):
         most = parts.at[step, pl.ds(0, devices - 1)]
         pltpu.make_async_copy(most, most, r_send.at[step]).wait()
-    coded_store.wait()
 
 
 def solution(mesh):
@@ -287,15 +314,14 @@
         coded, level = pl.pallas_call(
             functools.partial(kernel, slabs, pencils),
             out_shape=(jax.ShapeDtypeStruct(density.shape, jnp.float32), jax.ShapeDtypeStruct((1, LANES), jnp.float32)),
-            in_specs=[pl.BlockSpec(memory_space=pltpu.SMEM)] * 2 + [pl.BlockSpec(memory_space=pl.ANY)] * 2,
-            out_specs=(pl.BlockSpec(memory_space=pl.ANY), pl.BlockSpec(memory_space=pltpu.VMEM)),
+            in_specs=[pl.BlockSpec(memory_space=pltpu.SMEM)] * 2 + [pl.BlockSpec(memory_space=pltpu.HBM)] * 2,
+            out_specs=(pl.BlockSpec(memory_space=pltpu.VMEM), pl.BlockSpec(memory_space=pltpu.VMEM)),
             scratch_shapes=[
                 pltpu.VMEM((depth, wide, cols), jnp.float32),
                 pltpu.VMEM((depth, wide, cols), jnp.float32),
                 pltpu.VMEM((RADIUS, wide, cols), jnp.float32),
                 pltpu.VMEM((depth, rows, cols), jnp.int32),
                 pltpu.VMEM((depth, wide, cols), jnp.float32),
-                pltpu.VMEM((depth, rows, cols), jnp.float32),
                 pltpu.VMEM((cols, cols), jnp.bfloat16),
                 pltpu.VMEM((2, 8, LANES), jnp.float32),
                 pltpu.VMEM((ITERS, slabs * pencils, 2, LANES), jnp.float32),
@@ -303,14 +329,16 @@
                 pltpu.SemaphoreType.DMA((steps,)),
                 pltpu.SemaphoreType.DMA((steps,)),
                 pltpu.SemaphoreType.DMA((steps,)),
+                pltpu.SemaphoreType.DMA((steps,)),
+                pltpu.SemaphoreType.DMA((steps,)),
                 pltpu.SemaphoreType.DMA((3,)),
                 pltpu.SemaphoreType.DMA((3,)),
-                pltpu.SemaphoreType.DMA((3,)),
+                pltpu.SemaphoreType.DMA((2,)),
                 pltpu.SemaphoreType.DMA((ITERS,)),
                 pltpu.SemaphoreType.DMA((ITERS,)),
             ],
             compiler_params=pltpu.CompilerParams(
-                collective_id=0, has_side_effects=True, vmem_limit_bytes=40 * 1024 * 1024),
+                collective_id=0, has_side_effects=True, vmem_limit_bytes=49 * 1024 * 1024),
         )(sharpness, fraction, density, cell_kind)
         threshold = level[0, :1]
         physical = 0.5 * (1.0 + jnp.tanh(sharpness[0] * (coded - threshold[0])))

time: 117 us -> 110 us (0.940)
  Pallas kernels: 108 us -> 104 us
  local copies, waits for them, and re-layouts: 3.99 us -> 0 us
    unnamed x4 -> x0, local copies, waits for them, and re-layouts: 3.99 us -> none
    pallas_call x1, Pallas kernels: 108 us -> 104 us  [local(): pl.pallas_call(functools.partial(kernel, slabs, pencils), out_shape=(jax....]
where the time goes in v2:
time: 110 us
  Pallas kernels  104 us (95%)
  between operations  3.09 us (3%)
  other arithmetic  2.4 us (2%)
    pallas_call x1, Pallas kernels, local(): pl.pallas_call(functools.partial(kernel, slabs, pencils), out_shape=(jax....  104 us
    mul x1, other arithmetic, local(): physical = 0.5 * (1.0 + jnp.tanh(sharpness[0] * (coded - threshold[0])))  2.4 us

profile of v2, /device:TPU:0, one launch (start us, length us, event | category | flops | bytes accessed | tf_op | source)
XLA Modules:
  0.0 109.7 jit_solution(1774323178389460337)
XLA Ops:
  1.9 104.2 %shard_map.59 = (f32[6,384,384]{2,1,0:T(8,128)S(1)}, f32[1,128]{1,0:T(1,128)S(1)}) custom-call(f32[1]{0:T(128)} %copy.7.beta_ref, f32[1]{0:T(128)S(6)} %copy.8.fraction_ref, f32[6,384,384]{2,1,0:T(8,128)} %density.1, s32[6,384,384]{2,1,0:T(8,128)} %kind.1), custom_call_target="tpu_custom_call" | custom-call | tf_op jit(solution)/shard_map/pallas_call | solution.py:314
  106.1 2.4 %add_multiply_fusion = f32[6,384,384]{2,1,0:T(8,128)} fusion(f32[6,384,384]{2,1,0:T(8,128)S(1)} %get-tuple-element.4, f32[]{:T(128)S(1)} %bitcast.5, f32[]{:T(128)} %bitcast.4), kind=kLoop, calls=%fused_computation | loop fusion | flops 3538944 | bytes 7077896 | tf_op jit(solution)/shard_map/mul | solution.py:344

commit v3 on v2

--- a/solution.py
+++ b/solution.py
@@ -69,10 +69,15 @@
 
     barrier = pltpu.get_barrier_semaphore()
 
-    @pl.loop(1, devices)
-    def _(k):
-        other = (me + k) % devices
-        pl.semaphore_signal(barrier, inc=1, device_id=(other // pencils, other % pencils), device_id_type=MESH)
+    def greet(k, carry):
+        there = slab + (slabs - k)
+        there = there - jnp.where(there >= slabs, slabs, 0)
+        for core in range(pencils):
+            pl.semaphore_signal(barrier, inc=1, device_id=(there, core), device_id_type=MESH)
+        return carry
+
+    lax.fori_loop(1, slabs, greet, 0, unroll=15 if slabs % 15 == 1 else 1)
+    pl.semaphore_signal(barrier, inc=1, device_id=(slab, 1 - pencil), device_id_type=MESH)
 
     partner = slab + jnp.where(even, 1, -1)
     target = slab + jnp.where(even, 2, -2)
@@ -253,7 +258,7 @@
                 return total, bend
 
             zero = jnp.zeros((8, cols), jnp.float32)
-            total, bend = lax.fori_loop(0, rows // 8, body, (zero, zero))
+            total, bend = lax.fori_loop(0, rows // 8, body, (zero, zero), unroll=2)
             total, bend = folded(total), folded(bend)
         else:
             total, bend = acc[0], acc[1]
@@ -272,7 +277,7 @@
                 send(there, core)
             return carry
 
-        lax.fori_loop(1, slabs, send_all, 0, unroll=5 if slabs % 5 == 1 else 1)
+        lax.fori_loop(1, slabs, send_all, 0, unroll=15 if slabs % 15 == 1 else 1)
         send(slab, sibling)
 
         most = parts.at[step, pl.ds(0, devices - 1)]

time: 110 us -> 109 us (level)
  no operation moved by 1% of the time
where the time goes in v3:
time: 109 us
  Pallas kernels  103 us (94%)
  between operations  3.09 us (3%)
  other arithmetic  2.4 us (2%)
    pallas_call x1, Pallas kernels, local(): pl.pallas_call(functools.partial(kernel, slabs, pencils), out_shape=(jax....  103 us
    mul x1, other arithmetic, local(): physical = 0.5 * (1.0 + jnp.tanh(sharpness[0] * (coded - threshold[0])))  2.4 us

profile of v3, /device:TPU:0, one launch (start us, length us, event | category | flops | bytes accessed | tf_op | source)
XLA Modules:
  0.0 108.8 jit_solution(16735328512022405247)
XLA Ops:
  1.9 103.3 %shard_map.59 = (f32[6,384,384]{2,1,0:T(8,128)S(1)}, f32[1,128]{1,0:T(1,128)S(1)}) custom-call(f32[1]{0:T(128)} %copy.7.beta_ref, f32[1]{0:T(128)S(6)} %copy.8.fraction_ref, f32[6,384,384]{2,1,0:T(8,128)} %density.1, s32[6,384,384]{2,1,0:T(8,128)} %kind.1), custom_call_target="tpu_custom_call" | custom-call | tf_op jit(solution)/shard_map/pallas_call | solution.py:319
  105.2 2.4 %add_multiply_fusion = f32[6,384,384]{2,1,0:T(8,128)} fusion(f32[6,384,384]{2,1,0:T(8,128)S(1)} %get-tuple-element.4, f32[]{:T(128)S(1)} %bitcast.5, f32[]{:T(128)} %bitcast.4), kind=kLoop, calls=%fused_computation | loop fusion | flops 3538944 | bytes 7077896 | tf_op jit(solution)/shard_map/mul | solution.py:349
